TPU v7x, 512 devices: a whole 4x4x16 slice. The times are simulated.
512 devices in a mesh: dp: 4 (over y), row: 16 (over x, z_lo), col: 8 (over z_hi, core).
Axes of the slice: x: 4, y: 4, z: 16 (z_hi: 4, z_lo: 4; z = z_hi * 4 + z_lo), core: 2. Of those that a mesh axis runs over, the one named last changes fastest.
Arguments:
- grad_parts: float32 [4, 4, 1024, 10240], P('dp', None, 'row', 'col'), may hold values from -120 to 120, as said below
- gauss_noise: float32 [4096, 10240], P(('dp', 'row'), 'col'), may hold values from -6 to 6
- blt_buffers: float32 [4, 4096, 10240], P(None, ('dp', 'row'), 'col'), may hold values from -4 to 4
- blt_decays: float32 [4], replicated, may hold values from 0.2 to 0.98
- blt_weights: float32 [4], replicated, may hold values from 0.1 to 0.6
- master_weights: float32 [4096, 10240], P(('dp', 'row'), 'col'), may hold values from -4 to 4
- row_stat: float32 [4096], P(('dp', 'row')), may hold values from 0.05 to 0.5
- col_stat: float32 [10240], P('col'), may hold values from 0.05 to 0.5
Outputs:
- direction: float32 [4096, 10240], P(('dp', 'row'), 'col')
- weight_copy: bfloat16 [4096, 10240], P(('dp', 'row'), 'col')
- new_buffers: float32 [4, 4096, 10240], P(None, ('dp', 'row'), 'col')
- new_row_stat: float32 [4096], P(('dp', 'row'))
- new_col_stat: float32 [10240], P('col')
Inputs may be any that keep to these rules, and one draw needn't show every extreme that they name: `grad_parts`: finite real values.
All inputs are finite; a program needn't handle non-finite values.
Results may differ from a plain program's by a relative error of at most 0.001.
Values sent between devices are 32-bit elements; how exact they have to be, the bound alone decides.
No kernel may reach another device: no remote copies, remote signals or barrier semaphores. Data moves between devices by JAX's collectives and lax.ppermute only.
A program may use at most 64 MiB of HBM per device.

v0:
```python
import jax
import jax.numpy as jnp
from jax import lax
from jax.sharding import Mesh
from jax.sharding import PartitionSpec as P

D = 4096
FF = 10240
NOISE_STD = 2.0
DECAY_RATE = 0.85
LEARN_RATE = 0.01
TINY_TERM = 1e-30
ROW = ("x", "zl")
COL = ("zh", "core")
RUN = ("zl", "core")
PLANE = ("dp", "x")


def sum_of_sent(messages, axes):
    arrived = lax.all_to_all(messages, axes, split_axis=0, concat_axis=0, tiled=True)
    return arrived.sum(axis=0)


def per_device(
    grad_parts,
    gauss_noise,
    blt_buffers,
    blt_decays,
    blt_weights,
    master_weights,
    row_stat,
    col_stat,
):
    rows, cols = gauss_noise.shape
    n_col, n_run, n_plane = (lax.axis_size(axes) for axes in (COL, RUN, PLANE))
    arrived = lax.all_to_all(
        grad_parts.reshape(-1, rows, cols), "dp", split_axis=0, concat_axis=0, tiled=True
    )
    correlated = gauss_noise - jnp.sum(blt_buffers * blt_weights[:, None, None], axis=0)
    new_buffers = blt_decays[:, None, None] * blt_buffers + correlated[None]
    to = jnp.arange(n_run)
    same_cols = (to % 2 == lax.axis_index("core")).astype(jnp.float32)
    same_rows = (to // 2 == lax.axis_index("zl")).astype(jnp.float32)
    takes = jnp.concatenate(
        [
            jnp.broadcast_to(same_cols[:, None], (n_run, cols)),
            jnp.ones((n_run, rows), jnp.float32),
            jnp.broadcast_to(same_rows[:, None], (n_run, rows)),
        ],
        axis=1,
    )
    ones = jnp.broadcast_to(same_cols[0] + same_cols[1], (rows, rows))
    arrived, correlated, new_buffers, takes, row_stat, ones = lax.optimization_barrier(
        (arrived, correlated, new_buffers, takes, row_stat, ones)
    )
    noisy = arrived.sum(axis=0) + NOISE_STD * correlated
    squares = noisy * noisy
    share = DECAY_RATE / n_col * row_stat + (1.0 - DECAY_RATE) * (
        jnp.sum(squares, axis=1) / FF + TINY_TERM / n_col
    )
    sums = jnp.concatenate([jnp.sum(squares, axis=0), share, share])
    sums, col_stat, master_weights, takes = lax.optimization_barrier(
        (sums, col_stat, master_weights, takes)
    )
    run = sum_of_sent(sums[None] * takes, RUN)
    run, own = lax.optimization_barrier((run, run[cols + rows :]))
    plane = sum_of_sent(jnp.broadcast_to(run[None], (n_plane, *run.shape)), PLANE)
    stats = jnp.concatenate([plane[cols : cols + rows], own])
    new_col = DECAY_RATE * col_stat + (1.0 - DECAY_RATE) * (plane[:cols] / D + TINY_TERM)
    stats, new_col = lax.optimization_barrier((stats, new_col))
    stats = lax.psum(stats, "zh")
    shares, new_row = lax.optimization_barrier((stats[:rows], stats[rows:]))
    row_mean = jnp.sum(ones * shares[None, :], axis=1) / D
    direction = noisy / jnp.sqrt((new_row / row_mean)[:, None] * new_col[None, :])
    weight_copy = (master_weights - LEARN_RATE * direction).astype(jnp.bfloat16)
    return (direction, weight_copy, new_buffers, new_row, new_col)


def solution(mesh):
    finer = Mesh(
        mesh.devices.reshape(mesh.shape["dp"], 4, 4, 4, 2), ("dp", "x", "zl", "zh", "core")
    )
    rows = ("dp", *ROW)
    return jax.shard_map(
        per_device,
        mesh=finer,
        in_specs=(
            P("dp", None, ROW, COL),
            P(rows, COL),
            P(None, rows, COL),
            P(),
            P(),
            P(rows, COL),
            P(rows),
            P(COL),
        ),
        out_specs=(P(rows, COL), P(rows, COL), P(None, rows, COL), P(rows), P(COL)),
        check_vma=False,
    )
```

profile of v0, /device:TPU:2, one launch (start us, length us, event | category | flops | bytes accessed | tf_op | source)
XLA Modules:
  0.0 66.8 jit_solution(16642398468333567956)
XLA Ops:
  0.6 0.0 copy-start
  0.6 0.0 copy-start.5
  0.7 4.6 %all-to-all-start = ((f32[4,64,1280]{2,1,0:T(8,128)}), f32[4,64,1280]{2,1,0:T(8,128)S(1)}, u32[]{:S(2)}, u32[]{:S(2)}) async-start(f32[4,64,1280]{2,1,0:T(8,128)} %bitcast.2), calls=%async_computation | async-start | bytes 2621440 | tf_op jit(solution)/shard_map/all_to_all | solution.py:36
  5.3 0.0 copy-start.1
  5.3 0.6 fusion.4
  7.2 0.0 copy-done
  7.2 0.0 copy-done.5
  7.2 0.0 copy-start.6
  7.2 0.2 multiply_reduce_fusion
  7.3 0.0 copy-done.1
  7.4 0.1 broadcast_in_dim.12
  7.5 0.1 broadcast_in_dim.10
  7.6 0.1 concatenate.9
  7.6 0.2 copy-done.6
  7.8 1.2 %multiply_add_fusion = f32[4,64,1280]{2,1,0:T(8,128)} fusion(f32[4,64,1280]{2,1,0:T(8,128)S(1)} %copy-done, f32[64,1280]{1,0:T(8,128)S(1)} %sub.10, f32[4]{0:T(128)S(1)} %copy-done.6), kind=kLoop, calls=%fused_computation | loop fusion | flops 655360 | bytes 2949136 | tf_op jit(solution)/shard_map/add | solution.py:40
  9.1 0.0 copy-start.8
  9.1 14.1 %all-to-all-done = f32[4,64,1280]{2,1,0:T(8,128)S(1)} async-done(((f32[4,64,1280]{2,1,0:T(8,128)}), f32[4,64,1280]{2,1,0:T(8,128)S(1)}, u32[]{:S(2)}, u32[]{:S(2)}) %all-to-all-start) | async-done | bytes 1310752 | tf_op jit(solution)/shard_map/all_to_all | solution.py:36
  23.2 0.0 copy-start.4
  23.2 0.0 copy-start.2
  23.2 0.1 reduce_sum.64
  23.3 0.2 multiply_reduce_fusion.1
  23.4 0.0 copy-done.8
  23.4 0.1 concatenate.10
  23.6 11.5 %all_to_all.20 = f32[8,1,1408]{2,1,0:T(1,128)S(1)} all-to-all(f32[8,1,1408]{2,1,0:T(1,128)S(1)} %all_to_all.14), channel_id=1, replica_groups=mesh['dp'=4,'x'=4,'zl'=4,'zh'=4,'core'=2] {'zl','core'}, dimensions={0} | all-to-all | bytes 90112 | tf_op jit(solution)/shard_map/all_to_all | solution.py:20
  35.1 0.1 slice.28
  35.2 11.7 %all_to_all.21 = f32[16,1,1408]{2,1,0:T(1,128)S(1)} all-to-all(f32[16,1,1408]{2,1,0:T(1,128)S(1)} %broadcast_in_dim.14), channel_id=1, replica_groups=mesh['dp'=4,'x'=4,'zl'=4,'zh'=4,'core'=2] {'dp','x'}, dimensions={0} | all-to-all | bytes 180224 | tf_op jit(solution)/shard_map/all_to_all | solution.py:20
  46.9 0.1 reduce_sum.68
  47.0 0.0 copy-done.4
  47.0 0.0 copy-start.3
  47.0 0.1 pad_maximum_fusion
  47.1 18.5 %psum.7 = f32[128]{0:T(128)S(1)} all-reduce(f32[128]{0:T(128)S(1)} %pad_maximum_fusion), channel_id=1, replica_groups=mesh['dp'=4,'x'=4,'zl'=4,'zh'=4,'core'=2] {'zh'}, use_global_device_ids=true, to_apply=%region_6.7 | all-reduce | flops 128 | bytes 1024 | tf_op jit(solution)/shard_map/psum | solution.py:71
  65.6 0.1 fusion.3
  65.7 0.0 copy-start.7
  65.7 0.1 multiply_reduce_fusion.3
  65.8 0.0 copy-done.2
  65.8 0.9 %subtract_convert_fusion = (bf16[64,1280]{1,0:T(8,128)(2,1)}, f32[64,1280]{1,0:T(8,128)}) fusion(f32[64,1280]{1,0:T(8,128)S(1)} %copy-done.2, f32[1280]{0:T(1024)S(1)} %fusion.2, f32[64]{0:T(128)S(1)} %multiply_divide_fusion, f32[64,1280]{1,0:T(8,128)S(1)} %reduce_sum.64, f32[64,1280]{1,0:T(8,128)S(1)} %sub.10), kind=kLoop, calls=%fused_computation.2 | loop fusion | flops 573440 | bytes 1479936 | tf_op jit(solution)/shard_map/convert_element_type | solution.py:75
  66.8 0.0 copy-done.3
  66.8 0.0 copy-done.7
  (13 shorter events, 0.2 us)
Async XLA Ops:
  0.6 6.5 %copy-start = (f32[4,64,1280]{2,1,0:T(8,128)S(1)}, f32[4,64,1280]{2,1,0:T(8,128)}, u32[]{:S(2)}) copy-start(f32[4,64,1280]{2,1,0:T(8,128)} %param.10) | copy-start | bytes 3932164
  0.6 6.5 %copy-start.5 = (f32[4]{0:T(128)S(1)}, f32[4]{0:T(128)}, u32[]{:S(2)}) copy-start(f32[4]{0:T(128)} %param.12) | copy-start | bytes 52
  0.7 22.5 %all-to-all-start = ((f32[4,64,1280]{2,1,0:T(8,128)}), f32[4,64,1280]{2,1,0:T(8,128)S(1)}, u32[]{:S(2)}, u32[]{:S(2)}) async-start(f32[4,64,1280]{2,1,0:T(8,128)} %bitcast.2), calls=%async_computation | async-start | bytes 2621440 | tf_op jit(solution)/shard_map/all_to_all | solution.py:36
  5.3 2.1 %copy-start.1 = (f32[64,1280]{1,0:T(8,128)S(1)}, f32[64,1280]{1,0:T(8,128)}, u32[]{:S(2)}) copy-start(f32[64,1280]{1,0:T(8,128)} %param.9) | copy-start | bytes 983044
  7.2 0.7 copy-start.6
  9.1 14.4 %copy-start.8 = (f32[64]{0:T(128)S(1)}, f32[64]{0:T(128)}, u32[]{:S(2)}) copy-start(f32[64]{0:T(128)} %param.14) | copy-start | bytes 772
  23.2 23.8 %copy-start.4 = (f32[1280]{0:T(1024)S(1)}, f32[1280]{0:T(1024)}, u32[]{:S(2)}) copy-start(f32[1280]{0:T(1024)} %param.15) | copy-start | bytes 15364
  23.2 42.7 %copy-start.2 = (f32[64,1280]{1,0:T(8,128)S(1)}, f32[64,1280]{1,0:T(8,128)}, u32[]{:S(2)}) copy-start(f32[64,1280]{1,0:T(8,128)} %param.13) | copy-start | bytes 983044
  47.0 19.8 %copy-start.3 = (f32[1280]{0:T(1024)}, f32[1280]{0:T(1024)S(1)}, u32[]{:S(2)}) copy-start(f32[1280]{0:T(1024)S(1)} %fusion.2) | copy-start | bytes 15364
  65.7 1.1 %copy-start.7 = (f32[64]{0:T(128)}, f32[64]{0:T(128)S(1)}, u32[]{:S(2)}) copy-start(f32[64]{0:T(128)S(1)} %get-tuple-element.19) | copy-start | bytes 772
where the time goes:
time: 67.1 us; the launch traced here: 66.8 us
  blocking collectives  41.7 us (62%)
  waiting for transfers between devices  14.1 us (21%)
  starting transfers between devices  4.61 us (7%)
  other arithmetic  2.93 us (4%)
  between operations  2.1 us (3%)
  local copies, waits for them, and re-layouts  1.35 us (2%)
    all_to_all x2, blocking collectives, sum_of_sent(): lax.all_to_all(messages, axes, split_axis=0, concat_axis=0, tiled=True)  23.2 us
    psum x1, blocking collectives, per_device(): stats = lax.psum(stats, 'zh')  18.5 us
    all_to_all x1, waiting for transfers between devices, per_device(): lax.all_to_all(grad_parts.reshape(-1, rows, cols), 'dp', split_axis=0, co...  14.1 us
    all_to_all x1, starting transfers between devices, per_device(): lax.all_to_all(grad_parts.reshape(-1, rows, cols), 'dp', split_axis=0, co...  4.61 us
  transfers between devices with their start and end apart: 1, of which 1 were waited for; matrix products, arithmetic and copies ran while one was open for 3% of the time, Pallas kernels for 0%

commit v1 on v0

--- a/solution.py
+++ b/solution.py
@@ -14,6 +14,10 @@
 COL = ("zh", "core")
 RUN = ("zl", "core")
 PLANE = ("dp", "x")
+
+
+def hold_samples_all_for(own_rows):
+    return jnp.sum(lax.all_gather(own_rows, "zh"), axis=0)
 
 
 def sum_of_sent(messages, axes):
@@ -68,7 +72,7 @@
     stats = jnp.concatenate([plane[cols : cols + rows], own])
     new_col = DECAY_RATE * col_stat + (1.0 - DECAY_RATE) * (plane[:cols] / D + TINY_TERM)
     stats, new_col = lax.optimization_barrier((stats, new_col))
-    stats = lax.psum(stats, "zh")
+    stats = hold_samples_all_for(stats)
     shares, new_row = lax.optimization_barrier((stats[:rows], stats[rows:]))
     row_mean = jnp.sum(ones * shares[None, :], axis=1) / D
     direction = noisy / jnp.sqrt((new_row / row_mean)[:, None] * new_col[None, :])

time: 67.1 us -> 66.3 us (0.988)
  blocking collectives: 41.7 us -> 40.9 us
    psum x1 -> x0, blocking collectives: 18.5 us -> none  [per_device(): stats = lax.psum(stats, 'zh')]
    all_gather x0 -> x1, blocking collectives: none -> 17.8 us  [hold_samples_all_for(): return jnp.sum(lax.all_gather(own_rows, 'zh'), axis=0)]
where the time goes in v1:
time: 66.3 us; the launch traced here: 66 us
  blocking collectives  40.9 us (62%)
  waiting for transfers between devices  14.1 us (21%)
  starting transfers between devices  4.61 us (7%)
  other arithmetic  2.95 us (4%)
  between operations  2.1 us (3%)
  local copies, waits for them, and re-layouts  1.35 us (2%)
    all_to_all x2, blocking collectives, sum_of_sent(): lax.all_to_all(messages, axes, split_axis=0, concat_axis=0, tiled=True)  23.2 us
    all_gather x1, blocking collectives, hold_samples_all_for(): return jnp.sum(lax.all_gather(own_rows, 'zh'), axis=0)  17.8 us
    all_to_all x1, waiting for transfers between devices, per_device(): lax.all_to_all(grad_parts.reshape(-1, rows, cols), 'dp', split_axis=0, co...  14.1 us
    all_to_all x1, starting transfers between devices, per_device(): lax.all_to_all(grad_parts.reshape(-1, rows, cols), 'dp', split_axis=0, co...  4.61 us
  transfers between devices with their start and end apart: 1, of which 1 were waited for; matrix products, arithmetic and copies ran while one was open for 3% of the time, Pallas kernels for 0%

profile of v1, /device:TPU:2, one launch (start us, length us, event | category | flops | bytes accessed | tf_op | source)
XLA Modules:
  0.0 66.0 jit_solution(1717628756001904822)
XLA Ops:
  0.6 0.0 copy-start
  0.6 0.0 copy-start.5
  0.7 4.6 %all-to-all-start = ((f32[4,64,1280]{2,1,0:T(8,128)}), f32[4,64,1280]{2,1,0:T(8,128)S(1)}, u32[]{:S(2)}, u32[]{:S(2)}) async-start(f32[4,64,1280]{2,1,0:T(8,128)} %bitcast.3), calls=%async_computation | async-start | bytes 2621440 | tf_op jit(solution)/shard_map/all_to_all | solution.py:40
  5.3 0.0 copy-start.1
  5.3 0.6 fusion.4
  7.2 0.0 copy-done
  7.2 0.0 copy-done.5
  7.2 0.0 copy-start.6
  7.2 0.2 multiply_reduce_fusion
  7.3 0.0 copy-done.1
  7.4 0.1 broadcast_in_dim.12
  7.5 0.1 broadcast_in_dim.10
  7.6 0.1 concatenate.9
  7.6 0.2 copy-done.6
  7.8 1.2 %multiply_add_fusion = f32[4,64,1280]{2,1,0:T(8,128)} fusion(f32[4,64,1280]{2,1,0:T(8,128)S(1)} %copy-done, f32[64,1280]{1,0:T(8,128)S(1)} %sub.10, f32[4]{0:T(128)S(1)} %copy-done.6), kind=kLoop, calls=%fused_computation | loop fusion | flops 655360 | bytes 2949136 | tf_op jit(solution)/shard_map/add | solution.py:44
  9.1 0.0 copy-start.8
  9.1 14.1 %all-to-all-done = f32[4,64,1280]{2,1,0:T(8,128)S(1)} async-done(((f32[4,64,1280]{2,1,0:T(8,128)}), f32[4,64,1280]{2,1,0:T(8,128)S(1)}, u32[]{:S(2)}, u32[]{:S(2)}) %all-to-all-start) | async-done | bytes 1310752 | tf_op jit(solution)/shard_map/all_to_all | solution.py:40
  23.2 0.0 copy-start.4
  23.2 0.0 copy-start.2
  23.2 0.1 reduce_sum.73
  23.3 0.2 multiply_reduce_fusion.1
  23.4 0.0 copy-done.8
  23.4 0.1 concatenate.10
  23.6 11.5 %all_to_all.20 = f32[8,1,1408]{2,1,0:T(1,128)S(1)} all-to-all(f32[8,1,1408]{2,1,0:T(1,128)S(1)} %all_to_all.14), channel_id=1, replica_groups=mesh['dp'=4,'x'=4,'zl'=4,'zh'=4,'core'=2] {'zl','core'}, dimensions={0} | all-to-all | bytes 90112 | tf_op jit(solution)/shard_map/all_to_all | solution.py:24
  35.1 0.1 slice.28
  35.2 11.7 %all_to_all.21 = f32[16,1,1408]{2,1,0:T(1,128)S(1)} all-to-all(f32[16,1,1408]{2,1,0:T(1,128)S(1)} %broadcast_in_dim.14), channel_id=1, replica_groups=mesh['dp'=4,'x'=4,'zl'=4,'zh'=4,'core'=2] {'dp','x'}, dimensions={0} | all-to-all | bytes 180224 | tf_op jit(solution)/shard_map/all_to_all | solution.py:24
  46.9 0.1 reduce_sum.77
  47.0 0.0 copy-done.4
  47.0 0.0 copy-start.3
  47.0 0.1 pad_maximum_fusion
  47.1 17.8 %all-gather.1 = f32[4,1,128]{2,1,0:T(1,128)S(1)} all-gather(f32[1,1,128]{2,1,0:T(1,128)S(1)} %bitcast.4), channel_id=2, replica_groups=mesh['dp'=4,'x'=4,'zl'=4,'zh'=4,'core'=2] {'zh'}, dimensions={0}, use_global_device_ids=true | all-gather | bytes 2560 | tf_op jit(solution)/shard_map/all_gather | solution.py:20
  64.9 0.1 fusion.3
  65.0 0.0 copy-start.7
  65.0 0.1 multiply_reduce_fusion.3
  65.1 0.0 copy-done.2
  65.1 0.9 %subtract_convert_fusion = (bf16[64,1280]{1,0:T(8,128)(2,1)}, f32[64,1280]{1,0:T(8,128)}) fusion(f32[64,1280]{1,0:T(8,128)S(1)} %copy-done.2, f32[1280]{0:T(1024)S(1)} %fusion.2, f32[64]{0:T(128)S(1)} %multiply_divide_fusion, f32[64,1280]{1,0:T(8,128)S(1)} %reduce_sum.73, f32[64,1280]{1,0:T(8,128)S(1)} %sub.10), kind=kLoop, calls=%fused_computation.2 | loop fusion | flops 573440 | bytes 1479936 | tf_op jit(solution)/shard_map/convert_element_type | solution.py:79
  66.0 0.0 copy-done.3
  66.0 0.0 copy-done.7
  (14 shorter events, 0.2 us)
Async XLA Ops:
  0.6 6.5 %copy-start = (f32[4,64,1280]{2,1,0:T(8,128)S(1)}, f32[4,64,1280]{2,1,0:T(8,128)}, u32[]{:S(2)}) copy-start(f32[4,64,1280]{2,1,0:T(8,128)} %param.10) | copy-start | bytes 3932164
  0.6 6.5 %copy-start.5 = (f32[4]{0:T(128)S(1)}, f32[4]{0:T(128)}, u32[]{:S(2)}) copy-start(f32[4]{0:T(128)} %param.12) | copy-start | bytes 52
  0.7 22.5 %all-to-all-start = ((f32[4,64,1280]{2,1,0:T(8,128)}), f32[4,64,1280]{2,1,0:T(8,128)S(1)}, u32[]{:S(2)}, u32[]{:S(2)}) async-start(f32[4,64,1280]{2,1,0:T(8,128)} %bitcast.3), calls=%async_computation | async-start | bytes 2621440 | tf_op jit(solution)/shard_map/all_to_all | solution.py:40
  5.3 2.1 %copy-start.1 = (f32[64,1280]{1,0:T(8,128)S(1)}, f32[64,1280]{1,0:T(8,128)}, u32[]{:S(2)}) copy-start(f32[64,1280]{1,0:T(8,128)} %param.9) | copy-start | bytes 983044
  7.2 0.7 copy-start.6
  9.1 14.4 %copy-start.8 = (f32[64]{0:T(128)S(1)}, f32[64]{0:T(128)}, u32[]{:S(2)}) copy-start(f32[64]{0:T(128)} %param.14) | copy-start | bytes 772
  23.2 23.8 %copy-start.4 = (f32[1280]{0:T(1024)S(1)}, f32[1280]{0:T(1024)}, u32[]{:S(2)}) copy-start(f32[1280]{0:T(1024)} %param.15) | copy-start | bytes 15364
  23.2 41.9 %copy-start.2 = (f32[64,1280]{1,0:T(8,128)S(1)}, f32[64,1280]{1,0:T(8,128)}, u32[]{:S(2)}) copy-start(f32[64,1280]{1,0:T(8,128)} %param.13) | copy-start | bytes 983044
  47.0 19.0 %copy-start.3 = (f32[1280]{0:T(1024)}, f32[1280]{0:T(1024)S(1)}, u32[]{:S(2)}) copy-start(f32[1280]{0:T(1024)S(1)} %fusion.2) | copy-start | bytes 15364
  65.0 1.1 %copy-start.7 = (f32[64]{0:T(128)}, f32[64]{0:T(128)S(1)}, u32[]{:S(2)}) copy-start(f32[64]{0:T(128)S(1)} %get-tuple-element.19) | copy-start | bytes 772
